TPU v7x, 32 devices: a whole 2x2x4 slice. The times are simulated.
32 devices in a mesh: sp: 4 (over z), tp: 8 (over y, x, core).
Axes of the slice: x: 2, y: 2, z: 4, core: 2. Of those that a mesh axis runs over, the one named last changes fastest.
Arguments:
- tokens: bfloat16 [8192, 2048], P(('sp', 'tp')), may hold values from -3 to 3
- queries: bfloat16 [8192, 2048], P(('sp', 'tp')), may hold values from -140 to 140
- keys: bfloat16 [8192, 1024], P(('sp', 'tp')), may hold values from -6 to 6
- values: bfloat16 [8192, 1024], P(('sp', 'tp')), may hold values from -6 to 6
- out_weight: bfloat16 [2048, 2048], P('sp', 'tp'), may hold values from -0.25 to 0.25
- norm_gain: bfloat16 [2048], replicated, may hold values from 0.099609375 to 1.8984375
- gate_weight: bfloat16 [2048, 7168], P('sp', 'tp'), may hold values from -0.125 to 0.125
- up_weight: bfloat16 [2048, 7168], P('sp', 'tp'), may hold values from -0.125 to 0.125
- down_weight: bfloat16 [7168, 2048], P('tp', 'sp'), may hold values from -0.125 to 0.125
Outputs:
- attended: bfloat16 [8192, 2048], P(('sp', 'tp'))
- layer_out: bfloat16 [8192, 2048], P(('sp', 'tp'))
All inputs are finite; a program needn't handle non-finite values.
Results may differ from a plain program's by a relative error of at most 0.023.
Values may be sent and summed in bfloat16 or wider, within the bound.
A program may use at most 256 MiB of HBM per device.

v0:
```python
import functools
import math

import jax
import jax.numpy as jnp
from jax import lax
from jax.experimental import pallas as pl
from jax.experimental.pallas import tpu as pltpu
from jax.sharding import PartitionSpec as P

MESH = pl.DeviceIdType.MESH
HEAD_DIM = 128
KEY_CHUNK = 512
LOG2_SCALE = HEAD_DIM ** (-0.5) * math.log2(math.e)
norm_eps = 1e-05

GATE, UP, DOWN = 0, 1, 2


def layer_kernel(
    sp_count, tp_count,
    tok_ref, gain_ref, q_hbm, k_hbm, v_hbm, wo_hbm, gate_hbm, up_hbm, down_hbm,
    att_ref, out_ref,
    kv_all, q_all, qt_ref, acc_ref, attn_out, attn_full, wo_full, rows_all,
    gate_full, up_full, down_full, pair_buf, rs_buf,
    loc, kvz_s, kvz_r, qz_s, qz_r, woz_s, woz_r, az_s, az_r,
    pk_s, pk_r, pkf_s, pkf_r, pw_s, pw_r, pwf_s, pwf_r, pr_s, pr_r, prf_s, prf_r,
    w_s, w_r, pair_s, pair_r, rs_s, rs_r,
):
    S, T = sp_count, tp_count
    half = T // 2
    rows, D = tok_ref.shape
    HG = q_hbm.shape[1] // S
    KG = k_hbm.shape[1] // S
    DG = D // S
    WC = wo_hbm.shape[1]
    F = gate_hbm.shape[1]
    kv_local = KG // HEAD_DIM
    group = HG // KG
    width = group * rows
    segment_len = T * rows
    s = lax.axis_index("sp")
    t = lax.axis_index("tp")
    parity = lax.rem(t, 2)
    partner = t + 1 - 2 * parity

    def zpeer(d):
        return lax.rem(s + d, S)

    def tpeer(c):
        return lax.rem(t + 2 * c, T)

    def al(x, m):
        return pl.multiple_of(x, m)

    barrier = pltpu.get_barrier_semaphore()
    for d in range(1, S):
        pl.semaphore_signal(barrier, inc=1, device_id=(zpeer(d), t), device_id_type=MESH)
    for c in range(1, T):
        pl.semaphore_signal(
            barrier, inc=1, device_id=(s, lax.rem(t + c, T)), device_id_type=MESH
        )
    pl.semaphore_wait(barrier, S - 1 + T - 1)

    def remote(src, dst, ssem, rsem, ds, dt):
        return pltpu.make_async_remote_copy(
            src_ref=src, dst_ref=dst, send_sem=ssem, recv_sem=rsem,
            device_id=(ds, dt), device_id_type=MESH,
        )

    def kv_block(g, tt):
        return kv_all.at[pl.ds(al((g * T + tt) * rows, rows), rows), :]

    def kv_part(g, i):
        return kv_all.at[pl.ds(al((g * T + t) * rows, rows), rows), pl.ds(i * KG, KG)]

    def wo_piece(j):
        return wo_full.at[pl.ds(al(j * HG, HG), HG), pl.ds(al(t * WC, WC), WC)]

    def wo_block(tt):
        return wo_full.at[:, pl.ds(al(tt * WC, WC), WC)]

    def row_block(tt):
        return rows_all.at[pl.ds(al(tt * rows, rows), rows), :]

    fulls = (gate_full, up_full, down_full)
    owns = (gate_hbm, up_hbm, down_hbm)

    def w_slice(m, j):
        if m == DOWN:
            return down_full.at[:, pl.ds(al(j * DG, DG), DG)]
        return fulls[m].at[pl.ds(al(j * DG, DG), DG), :]

    def kvz(d, i):
        src = (k_hbm, v_hbm)[i].at[:, pl.ds(al(zpeer(d) * KG, KG), KG)]
        return remote(src, kv_part(s, i), kvz_s.at[d - 1, i], kvz_r.at[d - 1, i], zpeer(d), t)

    def qz(d):
        src = q_hbm.at[:, pl.ds(al(zpeer(d) * HG, HG), HG)]
        return remote(src, q_all.at[s], qz_s.at[d - 1], qz_r.at[d - 1], zpeer(d), t)

    def woz(d):
        return remote(wo_hbm, wo_piece(s), woz_s.at[d - 1], woz_r.at[d - 1], zpeer(d), t)

    kv_loc = [
        pltpu.make_async_copy(
            (k_hbm, v_hbm)[i].at[:, pl.ds(al(s * KG, KG), KG)], kv_part(s, i), loc.at[i]
        )
        for i in range(2)
    ]
    q_loc = pltpu.make_async_copy(
        q_hbm.at[:, pl.ds(al(s * HG, HG), HG)], q_all.at[s], loc.at[2]
    )
    wo_loc = pltpu.make_async_copy(wo_hbm, wo_piece(s), loc.at[3])
    w_loc = [
        pltpu.make_async_copy(owns[m], w_slice(m, s), loc.at[4 + m]) for m in range(3)
    ]

    def w_copy(m, d, side):
        j = s - d if side == 0 else s + d
        to = s + 1 if side == 0 else s - 1
        src = owns[m] if d == 0 else w_slice(m, j)
        return remote(src, w_slice(m, j), w_s.at[m, d, side], w_r.at[m, d, side], to, t)

    def w_sends(m, d, act):
        @pl.when(jnp.logical_and(s - d >= 0, s + 1 < S))
        def _():
            act(w_copy(m, d, 0))

        @pl.when(jnp.logical_and(s + d < S, s >= 1))
        def _():
            act(w_copy(m, d, 1))

    def w_wait(m, d):
        @pl.when(s - d >= 0)
        def _():
            j = s - d
            remote(
                w_slice(m, j), w_slice(m, j), w_s.at[m, d - 1, 0], w_r.at[m, d - 1, 0], s - 1, t
            ).wait_recv()

        @pl.when(s + d < S)
        def _():
            j = s + d
            remote(
                w_slice(m, j), w_slice(m, j), w_s.at[m, d - 1, 1], w_r.at[m, d - 1, 1], s + 1, t
            ).wait_recv()

    def start(copy):
        copy.start()

    for c in kv_loc:
        c.start()
    q_loc.start()
    wo_loc.start()
    for d in range(1, S):
        for i in range(2):
            kvz(d, i).start()
    for d in range(1, S):
        qz(d).start()
    for d in range(1, S):
        woz(d).start()
    for c in w_loc:
        c.start()
    for m in (GATE, UP, DOWN):
        w_sends(m, 0, start)

    def plane_send(block, ss, rs_, fs, fr):
        for c in range(1, half):
            remote(block(t), block(t), ss(c - 1), rs_(c - 1), s, tpeer(c)).start()
        remote(block(t), block(t), fs(0), fr(0), s, partner).start()

    def plane_forward(block, ss, rs_, fs, fr):
        for c in range(1, half):
            src = lax.rem(t - 2 * c + 2 * T, T)
            remote(block(src), block(src), ss(c - 1), rs_(c - 1), s, src).wait_recv()
            remote(block(src), block(src), fs(c), fr(c), s, partner).start()

    def plane_wait(block, ss, rs_, fs, fr):
        for c in range(half):
            src = lax.rem(partner - 2 * c + 2 * T, T)
            remote(block(src), block(src), fs(c), fr(c), s, partner).wait_recv()

    def plane_drain(block, ss, rs_, fs, fr):
        for c in range(1, half):
            remote(block(t), block(t), ss(c - 1), rs_(c - 1), s, tpeer(c)).wait_send()
        for c in range(half):
            remote(block(t), block(t), fs(c), fr(c), s, partner).wait_send()

    def kv_plane(g):
        return (
            lambda tt: kv_block(g, tt),
            lambda c: pk_s.at[g, c], lambda c: pk_r.at[g, c],
            lambda c: pkf_s.at[g, c], lambda c: pkf_r.at[g, c],
        )

    wo_plane = (
        wo_block,
        lambda c: pw_s.at[c], lambda c: pw_r.at[c],
        lambda c: pwf_s.at[c], lambda c: pwf_r.at[c],
    )
    row_plane = (
        row_block,
        lambda c: pr_s.at[c], lambda c: pr_r.at[c],
        lambda c: prf_s.at[c], lambda c: prf_r.at[c],
    )

    for c in kv_loc:
        c.wait()
    plane_send(*kv_plane(s))
    for g in range(S):
        @pl.when(s != g)
        def _():
            d = lax.rem(s - g + S, S)
            for i in range(2):
                remote(
                    kv_part(g, i), kv_part(g, i), kvz_s.at[d - 1, i], kvz_r.at[d - 1, i], g, t
                ).wait_recv()
            plane_send(*kv_plane(g))

    def attention(g):
        first_row = g * segment_len + t * rows
        for h in range(kv_local):
            for e in range(group):
                head = h * group + e
                qt_ref[h, :, e * rows : (e + 1) * rows] = q_all[
                    g, :, head * HEAD_DIM : (head + 1) * HEAD_DIM
                ].T
        acc_ref[...] = jnp.zeros_like(acc_ref)

        def step(chunk, carry, masked):
            first = al(chunk * KEY_CHUNK, KEY_CHUNK)
            scores = []
            for h in range(kv_local):
                k = kv_all[pl.ds(first, KEY_CHUNK), h * HEAD_DIM : (h + 1) * HEAD_DIM]
                sc = jnp.dot(k, qt_ref[h], preferred_element_type=jnp.float32)
                if masked:
                    key_pos = first + lax.broadcasted_iota(jnp.int32, (KEY_CHUNK, width), 0)
                    lane = lax.broadcasted_iota(jnp.int32, (KEY_CHUNK, width), 1)
                    sc = jnp.where(key_pos <= first_row + lax.rem(lane, rows), sc, -1e30)
                scores.append(sc)
            result = []
            for h in range(kv_local):
                peak, total = carry[h]
                sc = scores[h]
                new_peak = jnp.maximum(peak, jnp.max(sc, axis=0, keepdims=True))
                p = jnp.exp2((sc - new_peak) * LOG2_SCALE)
                fade = jnp.exp2((peak - new_peak) * LOG2_SCALE)
                total = total * fade + jnp.sum(p, axis=0, keepdims=True)
                v_at = KG + h * HEAD_DIM
                v = kv_all[pl.ds(first, KEY_CHUNK), v_at : v_at + HEAD_DIM]
                acc_ref[h] = acc_ref[h] * fade + lax.dot_general(
                    v, p.astype(jnp.bfloat16), (((0,), (0,)), ((), ())),
                    preferred_element_type=jnp.float32,
                )
                result.append((new_peak, total))
            return tuple(result)

        carry = tuple(
            (jnp.full((1, width), -1e30, jnp.float32), jnp.zeros((1, width), jnp.float32))
            for _ in range(kv_local)
        )
        whole_chunks = first_row // KEY_CHUNK
        carry = lax.fori_loop(0, whole_chunks, lambda i, c: step(i, c, False), carry)
        carry = step(whole_chunks, carry, True)
        for h in range(kv_local):
            mixed = (acc_ref[h] / carry[h][1]).astype(jnp.bfloat16)
            for e in range(group):
                head = h * group + e
                attn_out[g, :, head * HEAD_DIM : (head + 1) * HEAD_DIM] = mixed[
                    :, e * rows : (e + 1) * rows
                ].T

    def attn_copy(g):
        d = lax.rem(g - s + S, S)
        return remote(
            attn_out.at[g], attn_full.at[:, pl.ds(al(s * HG, HG), HG)],
            az_s.at[d - 1], az_r.at[d - 1], g, t,
        )

    def wo_z_wait():
        wo_loc.wait()
        for d in range(1, S):
            src = lax.rem(s - d + S, S)
            remote(wo_piece(src), wo_piece(src), woz_s.at[d - 1], woz_r.at[d - 1], src, t).wait_recv()

    plane_forward(*kv_plane(0))
    for g in range(S):
        if g + 1 < S:
            plane_forward(*kv_plane(g + 1))
        if g == min(1, S - 1):
            wo_z_wait()
            plane_send(*wo_plane)
        if g == S - 1:
            plane_forward(*wo_plane)

        @pl.when(s == g)
        def _():
            q_loc.wait()

        @pl.when(s != g)
        def _():
            d = lax.rem(s - g + S, S)
            remote(q_all.at[g], q_all.at[g], qz_s.at[d - 1], qz_r.at[d - 1], g, t).wait_recv()

        plane_wait(*kv_plane(g))
        attention(g)

        @pl.when(s == g)
        def _():
            attn_full[:, pl.ds(al(s * HG, HG), HG)] = attn_out[g]

        @pl.when(s != g)
        def _():
            attn_copy(g).start()

    for m in (GATE, UP):
        if S > 1:
            w_wait(m, 1)
        if S > 2:
            w_sends(m, 1, start)

    plane_wait(*wo_plane)
    for d in range(1, S):
        src = lax.rem(s - d + S, S)
        piece = attn_full.at[:, pl.ds(al(src * HG, HG), HG)]
        remote(piece, piece, az_s.at[d - 1], az_r.at[d - 1], src, t).wait_recv()

    tile = DG

    def project(n, squares):
        at = pl.ds(al(n * tile, tile), tile)
        total = jnp.dot(attn_full[...], wo_full[:, at], preferred_element_type=jnp.float32)
        a = (tok_ref[:, at].astype(jnp.float32) + total).astype(jnp.bfloat16)
        att_ref[:, at] = a
        wide = a.astype(jnp.float32)
        return squares + jnp.sum(wide * wide, axis=1, keepdims=True)

    squares = lax.fori_loop(0, S, project, jnp.zeros((rows, 1), jnp.float32))
    inverse_rms = lax.rsqrt(squares * (1.0 / D) + norm_eps)
    my_rows = pl.ds(al(t * rows, rows), rows)
    rows_all[my_rows, :] = (
        att_ref[...].astype(jnp.float32) * inverse_rms * gain_ref[...].astype(jnp.float32)
    ).astype(jnp.bfloat16)
    plane_send(*row_plane)

    for d in range(2, S - 1):
        for m in (GATE, UP):
            w_wait(m, d)
            w_sends(m, d, start)
    if S > 1:
        w_wait(DOWN, 1)
    if S > 2:
        w_sends(DOWN, 1, start)
    plane_forward(*row_plane)
    if S > 2:
        for m in (GATE, UP):
            w_wait(m, S - 1)
    w_loc[GATE].wait()
    w_loc[UP].wait()
    plane_wait(*row_plane)
    plane_drain(*wo_plane)
    for g in range(S):
        plane_drain(*kv_plane(g))

    step_rows = 2 * rows

    def hidden_step(b, _):
        at = pl.ds(al(b * step_rows, step_rows), step_rows)
        x = rows_all[at, :]
        gate = jnp.dot(x, gate_full[...], preferred_element_type=jnp.float32)
        up = jnp.dot(x, up_full[...], preferred_element_type=jnp.float32)
        wo_full[at, :F] = (gate / (1.0 + jnp.exp(-gate)) * up).astype(jnp.bfloat16)
        return 0

    lax.fori_loop(0, half, hidden_step, 0)

    near = jnp.minimum(s, S - 1 - s)

    def order(k):
        far = (k + 1) // 2
        swing = s - far if k % 2 else s + far
        tail = jnp.where(s == near, k, S - 1 - k)
        return jnp.where(k <= 2 * near, swing, tail)

    mine_base = S * half * rows

    def region(j, own):
        base = jnp.where(own, mine_base, 0)
        return base + j * (half * rows)

    def pair_copy(j):
        src = kv_all.at[pl.ds(al(region(j, False), rows), half * rows), :]
        return remote(src, pair_buf.at[j], pair_s.at[j], pair_r.at[j], s, partner)

    def rs_copy(j, c):
        block = lax.rem(t // 2 + c, half)
        src = kv_all.at[pl.ds(al(region(j, True) + block * rows, rows), rows), :]
        return remote(src, rs_buf.at[j, c - 1], rs_s.at[j, c - 1], rs_r.at[j, c - 1], s, tpeer(c))

    def down_step(j):
        cols = pl.ds(al(j * DG, DG), DG)

        def body(b, _):
            at = pl.ds(al(b * step_rows, step_rows), step_rows)
            y = jnp.dot(wo_full[at, :F], down_full[:, cols], preferred_element_type=jnp.float32)
            y = y.astype(jnp.bfloat16)
            for e in range(2):
                to = region(j, parity == e) + b * rows
                kv_all[pl.ds(al(to, rows), rows), :] = y[e * rows : (e + 1) * rows]
            return 0

        lax.fori_loop(0, half, body, 0)
        pair_copy(j).start()

    def reduce_step(j):
        pair_copy(j).wait_recv()
        for c in range(1, half):
            block = lax.rem(t // 2 + c, half)
            at = pl.ds(al(region(j, True) + block * rows, rows), rows)
            other = pair_buf[j, pl.ds(al(block * rows, rows), rows), :]
            kv_all[at, :] = (
                kv_all[at, :].astype(jnp.float32) + other.astype(jnp.float32)
            ).astype(jnp.bfloat16)
            rs_copy(j, c).start()

    w_loc[DOWN].wait()
    for k in range(S):
        j = order(k)
        dist = jnp.where(j < s, s - j, j - s)
        if k >= 1:
            for d in range(2, S):
                @pl.when(jnp.logical_and(dist == d, j < s))
                def _():
                    remote(
                        w_slice(DOWN, s - d), w_slice(DOWN, s - d),
                        w_s.at[DOWN, d - 1, 0], w_r.at[DOWN, d - 1, 0], s - 1, t,
                    ).wait_recv()
                    if d < S - 1:
                        @pl.when(s + 1 < S)
                        def _():
                            w_copy(DOWN, d, 0).start()

                @pl.when(jnp.logical_and(dist == d, j > s))
                def _():
                    remote(
                        w_slice(DOWN, s + d), w_slice(DOWN, s + d),
                        w_s.at[DOWN, d - 1, 1], w_r.at[DOWN, d - 1, 1], s + 1, t,
                    ).wait_recv()
                    if d < S - 1:
                        @pl.when(s >= 1)
                        def _():
                            w_copy(DOWN, d, 1).start()
        down_step(j)
        if k >= 1:
            reduce_step(order(k - 1))
    reduce_step(order(S - 1))

    mine = t // 2
    for k in range(S):
        j = order(k)
        cols = pl.ds(al(j * DG, DG), DG)
        for c in range(1, half):
            rs_copy(j, c).wait_recv()
        at = pl.ds(al(region(j, True) + mine * rows, rows), rows)
        total = att_ref[:, cols].astype(jnp.float32)
        total += kv_all[at, :].astype(jnp.float32)
        total += pair_buf[j, pl.ds(al(mine * rows, rows), rows), :].astype(jnp.float32)
        for c in range(1, half):
            total += rs_buf[j, c - 1].astype(jnp.float32)
        out_ref[:, cols] = total.astype(jnp.bfloat16)

    for d in range(1, S):
        for i in range(2):
            kvz(d, i).wait_send()
        qz(d).wait_send()
        woz(d).wait_send()
    for g in range(S):
        @pl.when(s != g)
        def _():
            attn_copy(g).wait_send()
    for m in (GATE, UP, DOWN):
        for d in range(S - 1):
            w_sends(m, d, lambda copy: copy.wait_send())
    plane_drain(*row_plane)
    for j in range(S):
        pair_copy(j).wait_send()
        for c in range(1, half):
            rs_copy(j, c).wait_send()


def shards(
    tokens, queries, keys, values, out_weight, norm_gain, gate_weight, up_weight, down_weight
):
    S = lax.axis_size("sp")
    T = lax.axis_size("tp")
    rows, D = tokens.shape
    HG = queries.shape[1] // S
    KG = keys.shape[1] // S
    DG = D // S
    F = gate_weight.shape[1]
    half = T // 2
    kv_local = KG // HEAD_DIM
    width = HG // KG * rows
    assert T % 2 == 0 and 2 * KG == DG and T * rows == S * HG and F <= D
    bf16, f32 = jnp.bfloat16, jnp.float32
    vmem, any_ = pl.BlockSpec(memory_space=pltpu.VMEM), pl.BlockSpec(memory_space=pl.ANY)
    sem = pltpu.SemaphoreType.DMA
    line = S - 1
    return pl.pallas_call(
        functools.partial(layer_kernel, S, T),
        out_shape=(
            jax.ShapeDtypeStruct((rows, D), bf16),
            jax.ShapeDtypeStruct((rows, D), bf16),
        ),
        in_specs=[vmem, vmem] + [any_] * 7,
        out_specs=(vmem, vmem),
        scratch_shapes=[
            pltpu.VMEM((S * T * rows, 2 * KG), bf16),
            pltpu.VMEM((S, rows, HG), bf16),
            pltpu.VMEM((kv_local, HEAD_DIM, width), bf16),
            pltpu.VMEM((kv_local, HEAD_DIM, width), f32),
            pltpu.VMEM((S, rows, HG), bf16),
            pltpu.VMEM((rows, S * HG), bf16),
            pltpu.VMEM((S * HG, D), bf16),
            pltpu.VMEM((T * rows, D), bf16),
            pltpu.VMEM((D, F), bf16),
            pltpu.VMEM((D, F), bf16),
            pltpu.VMEM((F, D), bf16),
            pltpu.VMEM((S, half * rows, DG), bf16),
            pltpu.VMEM((S, half - 1, rows, DG), bf16),
            sem((7,)),
            sem((line, 2)), sem((line, 2)), sem((line,)), sem((line,)),
            sem((line,)), sem((line,)), sem((line,)), sem((line,)),
            sem((S, half - 1)), sem((S, half - 1)), sem((S, half)), sem((S, half)),
            sem((half - 1,)), sem((half - 1,)), sem((half,)), sem((half,)),
            sem((half - 1,)), sem((half - 1,)), sem((half,)), sem((half,)),
            sem((3, line, 2)), sem((3, line, 2)),
            sem((S,)), sem((S,)), sem((S, half - 1)), sem((S, half - 1)),
        ],
        compiler_params=pltpu.CompilerParams(
            collective_id=0,
            has_side_effects=True,
            vmem_limit_bytes=67_043_328,
        ),
    )(
        tokens, norm_gain.reshape(1, D), queries, keys, values, out_weight,
        gate_weight, up_weight, down_weight,
    )


def solution(mesh):
    return jax.shard_map(
        shards,
        mesh=mesh,
        in_specs=(
            P(("sp", "tp"), None),
            P(("sp", "tp"), None),
            P(("sp", "tp"), None),
            P(("sp", "tp"), None),
            P("sp", "tp"),
            P(),
            P("sp", "tp"),
            P("sp", "tp"),
            P("tp", "sp"),
        ),
        out_specs=(P(("sp", "tp"), None), P(("sp", "tp"), None)),
        check_vma=False,
    )
```

profile of v0, /device:TPU:0, one launch (start us, length us, event | category | flops | bytes accessed | tf_op | source)
XLA Modules:
  0.0 303.8 jit_solution(3993294758017059230)
XLA Ops:
  0.6 1.3 reshape.7.gain_ref
  1.9 298.5 %shard_map.104 = (bf16[256,2048]{1,0:T(8,128)(2,1)}, bf16[256,2048]{1,0:T(8,128)(2,1)}) custom-call(bf16[256,2048]{1,0:T(8,128)(2,1)} %tok_ref.1, bf16[1,2048]{1,0:T(2,128)(2,1)} %reshape.7.gain_ref, bf16[256,2048]{1,0:T(8,128)(2,1)} %q_hbm.1, bf16[256,1024]{1,0:T(8,128)(2,1)} %k_hbm.1, bf16[256,1024]{1,0:T(8,128)(2,1)} %v_hbm.1, bf16[512,256]{1,0:T(8,128)(2,1)} %wo_hbm.1, ...), custom_call_target="tpu_custom_call" | custom-call | tf_op jit(solution)/shard_map/pallas_call | solution.py:510
  300.5 0.0 copy-start
  300.5 2.4 copy.13
  302.9 0.0 copy-done
  302.9 1.0 copy.14
Async XLA Ops:
  300.5 2.4 copy-start
where the time goes:
time: 307 us; the launch traced here: 304 us
  Pallas kernels  299 us (97%)
  local copies, waits for them, and re-layouts  4.66 us (2%)
    pallas_call x1, Pallas kernels, shards(): pl.pallas_call(functools.partial(layer_kernel, S, T), out_shape=(jax.Shap...  299 us

commit v1 on v0

--- a/solution.py
+++ b/solution.py
@@ -15,6 +15,12 @@
 norm_eps = 1e-05
 
 GATE, UP, DOWN = 0, 1, 2
+PARTS = 4
+LAG = 5
+
+
+def parts_of(columns):
+    return min(PARTS, columns // 128)
 
 
 def layer_kernel(
@@ -33,6 +39,8 @@
     HG = q_hbm.shape[1] // S
     KG = k_hbm.shape[1] // S
     DG = D // S
+    SUB = parts_of(DG)
+    SW = DG // SUB
     WC = wo_hbm.shape[1]
     F = gate_hbm.shape[1]
     kv_local = KG // HEAD_DIM
@@ -83,13 +91,15 @@
     def row_block(tt):
         return rows_all.at[pl.ds(al(tt * rows, rows), rows), :]
 
-    fulls = (gate_full, up_full, down_full)
-    owns = (gate_hbm, up_hbm, down_hbm)
+    def w_own(m):
+        if m >= DOWN:
+            return down_hbm.at[:, pl.ds((m - DOWN) * SW, SW)]
+        return (gate_hbm, up_hbm)[m]
 
     def w_slice(m, j):
-        if m == DOWN:
-            return down_full.at[:, pl.ds(al(j * DG, DG), DG)]
-        return fulls[m].at[pl.ds(al(j * DG, DG), DG), :]
+        if m >= DOWN:
+            return down_full.at[:, pl.ds(al(j * DG + (m - DOWN) * SW, SW), SW)]
+        return (gate_full, up_full)[m].at[pl.ds(al(j * DG, DG), DG), :]
 
     def kvz(d, i):
         src = (k_hbm, v_hbm)[i].at[:, pl.ds(al(zpeer(d) * KG, KG), KG)]
@@ -113,13 +123,13 @@
     )
     wo_loc = pltpu.make_async_copy(wo_hbm, wo_piece(s), loc.at[3])
     w_loc = [
-        pltpu.make_async_copy(owns[m], w_slice(m, s), loc.at[4 + m]) for m in range(3)
+        pltpu.make_async_copy(w_own(m), w_slice(m, s), loc.at[4 + m]) for m in range(2 + SUB)
     ]
 
     def w_copy(m, d, side):
         j = s - d if side == 0 else s + d
         to = s + 1 if side == 0 else s - 1
-        src = owns[m] if d == 0 else w_slice(m, j)
+        src = w_own(m) if d == 0 else w_slice(m, j)
         return remote(src, w_slice(m, j), w_s.at[m, d, side], w_r.at[m, d, side], to, t)
 
     def w_sends(m, d, act):
@@ -131,23 +141,35 @@
         def _():
             act(w_copy(m, d, 1))
 
-    def w_wait(m, d):
-        @pl.when(s - d >= 0)
-        def _():
-            j = s - d
-            remote(
-                w_slice(m, j), w_slice(m, j), w_s.at[m, d - 1, 0], w_r.at[m, d - 1, 0], s - 1, t
-            ).wait_recv()
-
-        @pl.when(s + d < S)
-        def _():
-            j = s + d
-            remote(
-                w_slice(m, j), w_slice(m, j), w_s.at[m, d - 1, 1], w_r.at[m, d - 1, 1], s + 1, t
-            ).wait_recv()
-
-    def start(copy):
-        copy.start()
+    def w_arrival(m, d, side):
+        j = s - d if side == 0 else s + d
+        sender = s - 1 if side == 0 else s + 1
+        return remote(
+            w_slice(m, j), w_slice(m, j),
+            w_s.at[m, d - 1, side], w_r.at[m, d - 1, side], sender, t,
+        )
+
+    def w_pass(m, d):
+        @pl.when(jnp.logical_and(s - d >= 0, s + 1 < S))
+        def _():
+            if d > 0:
+                w_arrival(m, d, 0).wait_recv()
+            w_copy(m, d, 0).start()
+
+        @pl.when(jnp.logical_and(s + d < S, s >= 1))
+        def _():
+            if d > 0:
+                w_arrival(m, d, 1).wait_recv()
+            w_copy(m, d, 1).start()
+
+    def w_rest(m, d):
+        @pl.when(s == S - 1)
+        def _():
+            w_arrival(m, d, 0).wait_recv()
+
+        @pl.when(s == 0)
+        def _():
+            w_arrival(m, d, 1).wait_recv()
 
     for c in kv_loc:
         c.start()
@@ -158,32 +180,66 @@
             kvz(d, i).start()
     for d in range(1, S):
         qz(d).start()
-    for d in range(1, S):
-        woz(d).start()
     for c in w_loc:
         c.start()
-    for m in (GATE, UP, DOWN):
-        w_sends(m, 0, start)
+
+    square = half == 4
+    tx = t + 2 - 4 * lax.rem(t // 2, 2)
+    ty = t + 4 - 8 * lax.rem(t // 4, 2)
+    td = tx + ty - t
+    if square:
+        sources = (t, tx, ty, td)
+    else:
+        sources = tuple(lax.rem(t - 2 * c + 2 * T, T) for c in range(half))
+
+    def part_of(block, i):
+        size = block.shape[0] // 2
+        return block.at[pl.ds(i * size, size), :]
 
     def plane_send(block, ss, rs_, fs, fr):
+        if square:
+            remote(block(t), block(t), ss(0), rs_(0), s, tx).start()
+            remote(block(t), block(t), ss(1), rs_(1), s, ty).start()
+        else:
+            for c in range(1, half):
+                remote(block(t), block(t), ss(c - 1), rs_(c - 1), s, tpeer(c)).start()
+        remote(block(t), block(t), fs(0), fr(0), s, partner).start()
+
+    def plane_forward(block, ss, rs_, fs, fr):
+        if square:
+            for i, (src, to) in enumerate(((tx, ty), (ty, tx))):
+                remote(block(src), block(src), ss(i), rs_(i), s, src).wait_recv()
+                piece = part_of(block(src), i)
+                remote(piece, piece, ss(2 + i), rs_(2 + i), s, to).start()
+                remote(block(src), block(src), fs(1 + i), fr(1 + i), s, partner).start()
+            return
         for c in range(1, half):
-            remote(block(t), block(t), ss(c - 1), rs_(c - 1), s, tpeer(c)).start()
-        remote(block(t), block(t), fs(0), fr(0), s, partner).start()
-
-    def plane_forward(block, ss, rs_, fs, fr):
-        for c in range(1, half):
-            src = lax.rem(t - 2 * c + 2 * T, T)
+            src = sources[c]
             remote(block(src), block(src), ss(c - 1), rs_(c - 1), s, src).wait_recv()
             remote(block(src), block(src), fs(c), fr(c), s, partner).start()
 
+    def plane_corner(block, ss, rs_, fs, fr):
+        if square:
+            for i, src in enumerate((ty, tx)):
+                piece = part_of(block(td), i)
+                remote(piece, piece, ss(2 + i), rs_(2 + i), s, src).wait_recv()
+            remote(block(td), block(td), fs(3), fr(3), s, partner).start()
+
     def plane_wait(block, ss, rs_, fs, fr):
         for c in range(half):
-            src = lax.rem(partner - 2 * c + 2 * T, T)
+            src = sources[c] + partner - t if square else lax.rem(partner - 2 * c + 2 * T, T)
             remote(block(src), block(src), fs(c), fr(c), s, partner).wait_recv()
 
     def plane_drain(block, ss, rs_, fs, fr):
-        for c in range(1, half):
-            remote(block(t), block(t), ss(c - 1), rs_(c - 1), s, tpeer(c)).wait_send()
+        if square:
+            for i, to in enumerate((tx, ty)):
+                remote(block(t), block(t), ss(i), rs_(i), s, to).wait_send()
+            for i, to in enumerate((ty, tx)):
+                piece = part_of(block(t), i)
+                remote(piece, piece, ss(2 + i), rs_(2 + i), s, to).wait_send()
+        else:
+            for c in range(1, half):
+                remote(block(t), block(t), ss(c - 1), rs_(c - 1), s, tpeer(c)).wait_send()
         for c in range(half):
             remote(block(t), block(t), fs(c), fr(c), s, partner).wait_send()
 
@@ -284,15 +340,18 @@
             src = lax.rem(s - d + S, S)
             remote(wo_piece(src), wo_piece(src), woz_s.at[d - 1], woz_r.at[d - 1], src, t).wait_recv()
 
+    for d in range(1, S):
+        woz(d).start()
+    for m in (GATE, UP):
+        w_pass(m, 0)
     plane_forward(*kv_plane(0))
     for g in range(S):
         if g + 1 < S:
             plane_forward(*kv_plane(g + 1))
-        if g == min(1, S - 1):
+        plane_corner(*kv_plane(g))
+        if g == S - 1:
             wo_z_wait()
             plane_send(*wo_plane)
-        if g == S - 1:
-            plane_forward(*wo_plane)
 
         @pl.when(s == g)
         def _():
@@ -314,11 +373,11 @@
         def _():
             attn_copy(g).start()
 
+    plane_forward(*wo_plane)
     for m in (GATE, UP):
-        if S > 1:
-            w_wait(m, 1)
         if S > 2:
-            w_sends(m, 1, start)
+            w_pass(m, 1)
+    plane_corner(*wo_plane)
 
     plane_wait(*wo_plane)
     for d in range(1, S):
@@ -340,22 +399,23 @@
     inverse_rms = lax.rsqrt(squares * (1.0 / D) + norm_eps)
     my_rows = pl.ds(al(t * rows, rows), rows)
     rows_all[my_rows, :] = (
-        att_ref[...].astype(jnp.float32) * inverse_rms * gain_ref[...].astype(jnp.float32)
+        att_ref[...].astype(jnp.float32) * inverse_rms * gain_ref[...].reshape(1, D).astype(jnp.float32)
     ).astype(jnp.bfloat16)
     plane_send(*row_plane)
 
     for d in range(2, S - 1):
+        w_pass(GATE, d)
+        if d == 2:
+            plane_forward(*row_plane)
+        w_pass(UP, d)
+    if S <= 3:
+        plane_forward(*row_plane)
+    for m in range(DOWN, DOWN + SUB):
+        w_pass(m, 0)
+    plane_corner(*row_plane)
+    for d in range(1, S):
         for m in (GATE, UP):
-            w_wait(m, d)
-            w_sends(m, d, start)
-    if S > 1:
-        w_wait(DOWN, 1)
-    if S > 2:
-        w_sends(DOWN, 1, start)
-    plane_forward(*row_plane)
-    if S > 2:
-        for m in (GATE, UP):
-            w_wait(m, S - 1)
+            w_rest(m, d)
     w_loc[GATE].wait()
     w_loc[UP].wait()
     plane_wait(*row_plane)
@@ -389,17 +449,21 @@
         base = jnp.where(own, mine_base, 0)
         return base + j * (half * rows)
 
-    def pair_copy(j):
-        src = kv_all.at[pl.ds(al(region(j, False), rows), half * rows), :]
-        return remote(src, pair_buf.at[j], pair_s.at[j], pair_r.at[j], s, partner)
-
-    def rs_copy(j, c):
+    def pair_copy(j, h):
+        at = pl.ds(al(region(j, False), rows), half * rows)
+        src = kv_all.at[at, pl.ds(h * SW, SW)]
+        return remote(src, pair_buf.at[j, h], pair_s.at[j, h], pair_r.at[j, h], s, partner)
+
+    def rs_copy(j, h, c):
         block = lax.rem(t // 2 + c, half)
-        src = kv_all.at[pl.ds(al(region(j, True) + block * rows, rows), rows), :]
-        return remote(src, rs_buf.at[j, c - 1], rs_s.at[j, c - 1], rs_r.at[j, c - 1], s, tpeer(c))
-
-    def down_step(j):
-        cols = pl.ds(al(j * DG, DG), DG)
+        at = pl.ds(al(region(j, True) + block * rows, rows), rows)
+        src = kv_all.at[at, pl.ds(h * SW, SW)]
+        return remote(
+            src, rs_buf.at[j, h, c - 1], rs_s.at[j, h, c - 1], rs_r.at[j, h, c - 1], s, tpeer(c)
+        )
+
+    def down_step(j, h):
+        cols = pl.ds(al(j * DG + h * SW, SW), SW)
 
         def body(b, _):
             at = pl.ds(al(b * step_rows, step_rows), step_rows)
@@ -407,68 +471,60 @@
             y = y.astype(jnp.bfloat16)
             for e in range(2):
                 to = region(j, parity == e) + b * rows
-                kv_all[pl.ds(al(to, rows), rows), :] = y[e * rows : (e + 1) * rows]
+                kv_all[pl.ds(al(to, rows), rows), h * SW : (h + 1) * SW] = y[
+                    e * rows : (e + 1) * rows
+                ]
             return 0
 
         lax.fori_loop(0, half, body, 0)
-        pair_copy(j).start()
-
-    def reduce_step(j):
-        pair_copy(j).wait_recv()
+        pair_copy(j, h).start()
+
+    def reduce_step(j, h):
+        pair_copy(j, h).wait_recv()
         for c in range(1, half):
             block = lax.rem(t // 2 + c, half)
             at = pl.ds(al(region(j, True) + block * rows, rows), rows)
-            other = pair_buf[j, pl.ds(al(block * rows, rows), rows), :]
-            kv_all[at, :] = (
-                kv_all[at, :].astype(jnp.float32) + other.astype(jnp.float32)
+            cols = slice(h * SW, (h + 1) * SW)
+            other = pair_buf[j, h, pl.ds(al(block * rows, rows), rows), :]
+            kv_all[at, cols] = (
+                kv_all[at, cols].astype(jnp.float32) + other.astype(jnp.float32)
             ).astype(jnp.bfloat16)
-            rs_copy(j, c).start()
-
-    w_loc[DOWN].wait()
-    for k in range(S):
-        j = order(k)
-        dist = jnp.where(j < s, s - j, j - s)
-        if k >= 1:
-            for d in range(2, S):
-                @pl.when(jnp.logical_and(dist == d, j < s))
-                def _():
-                    remote(
-                        w_slice(DOWN, s - d), w_slice(DOWN, s - d),
-                        w_s.at[DOWN, d - 1, 0], w_r.at[DOWN, d - 1, 0], s - 1, t,
-                    ).wait_recv()
-                    if d < S - 1:
-                        @pl.when(s + 1 < S)
-                        def _():
-                            w_copy(DOWN, d, 0).start()
-
-                @pl.when(jnp.logical_and(dist == d, j > s))
-                def _():
-                    remote(
-                        w_slice(DOWN, s + d), w_slice(DOWN, s + d),
-                        w_s.at[DOWN, d - 1, 1], w_r.at[DOWN, d - 1, 1], s + 1, t,
-                    ).wait_recv()
-                    if d < S - 1:
-                        @pl.when(s >= 1)
-                        def _():
-                            w_copy(DOWN, d, 1).start()
-        down_step(j)
-        if k >= 1:
-            reduce_step(order(k - 1))
-    reduce_step(order(S - 1))
+            rs_copy(j, h, c).start()
 
     mine = t // 2
-    for k in range(S):
-        j = order(k)
-        cols = pl.ds(al(j * DG, DG), DG)
+
+    def finish(j, h):
+        cols = pl.ds(al(j * DG + h * SW, SW), SW)
         for c in range(1, half):
-            rs_copy(j, c).wait_recv()
+            rs_copy(j, h, c).wait_recv()
         at = pl.ds(al(region(j, True) + mine * rows, rows), rows)
         total = att_ref[:, cols].astype(jnp.float32)
-        total += kv_all[at, :].astype(jnp.float32)
-        total += pair_buf[j, pl.ds(al(mine * rows, rows), rows), :].astype(jnp.float32)
+        total += kv_all[at, h * SW : (h + 1) * SW].astype(jnp.float32)
+        total += pair_buf[j, h, pl.ds(al(mine * rows, rows), rows), :].astype(jnp.float32)
         for c in range(1, half):
-            total += rs_buf[j, c - 1].astype(jnp.float32)
+            total += rs_buf[j, h, c - 1].astype(jnp.float32)
         out_ref[:, cols] = total.astype(jnp.bfloat16)
+
+    steps = [(k, h) for k in range(S) for h in range(SUB)]
+    for i, (k, h) in enumerate(steps):
+        j = order(k)
+        if h == 0 and 1 <= max(k, 1) < S - 1 and k != 1:
+            for m in range(DOWN, DOWN + SUB):
+                w_pass(m, max(k, 1))
+        if k >= 1:
+            w_rest(DOWN + h, k)
+        elif h == 0:
+            for m in range(DOWN, DOWN + SUB):
+                w_loc[m].wait()
+        down_step(j, h)
+        if i >= 1:
+            reduce_step(order(steps[i - 1][0]), steps[i - 1][1])
+        if i >= LAG:
+            finish(order(steps[i - LAG][0]), steps[i - LAG][1])
+    k, h = steps[-1]
+    reduce_step(order(k), h)
+    for k, h in steps[max(len(steps) - LAG, 0):]:
+        finish(order(k), h)
 
     for d in range(1, S):
         for i in range(2):
@@ -479,14 +535,15 @@
         @pl.when(s != g)
         def _():
             attn_copy(g).wait_send()
-    for m in (GATE, UP, DOWN):
+    for m in range(DOWN + SUB):
         for d in range(S - 1):
             w_sends(m, d, lambda copy: copy.wait_send())
     plane_drain(*row_plane)
     for j in range(S):
-        pair_copy(j).wait_send()
-        for c in range(1, half):
-            rs_copy(j, c).wait_send()
+        for h in range(SUB):
+            pair_copy(j, h).wait_send()
+            for c in range(1, half):
+                rs_copy(j, h, c).wait_send()
 
 
 def shards(
@@ -500,6 +557,7 @@
     DG = D // S
     F = gate_weight.shape[1]
     half = T // 2
+    SUB = parts_of(DG)
     kv_local = KG // HEAD_DIM
     width = HG // KG * rows
     assert T % 2 == 0 and 2 * KG == DG and T * rows == S * HG and F <= D
@@ -507,6 +565,7 @@
     vmem, any_ = pl.BlockSpec(memory_space=pltpu.VMEM), pl.BlockSpec(memory_space=pl.ANY)
     sem = pltpu.SemaphoreType.DMA
     line = S - 1
+    links = 4 if half == 4 else half - 1
     return pl.pallas_call(
         functools.partial(layer_kernel, S, T),
         out_shape=(
@@ -527,16 +586,16 @@
             pltpu.VMEM((D, F), bf16),
             pltpu.VMEM((D, F), bf16),
             pltpu.VMEM((F, D), bf16),
-            pltpu.VMEM((S, half * rows, DG), bf16),
-            pltpu.VMEM((S, half - 1, rows, DG), bf16),
-            sem((7,)),
+            pltpu.VMEM((S, SUB, half * rows, DG // SUB), bf16),
+            pltpu.VMEM((S, SUB, half - 1, rows, DG // SUB), bf16),
+            sem((6 + SUB,)),
             sem((line, 2)), sem((line, 2)), sem((line,)), sem((line,)),
             sem((line,)), sem((line,)), sem((line,)), sem((line,)),
-            sem((S, half - 1)), sem((S, half - 1)), sem((S, half)), sem((S, half)),
-            sem((half - 1,)), sem((half - 1,)), sem((half,)), sem((half,)),
-            sem((half - 1,)), sem((half - 1,)), sem((half,)), sem((half,)),
-            sem((3, line, 2)), sem((3, line, 2)),
-            sem((S,)), sem((S,)), sem((S, half - 1)), sem((S, half - 1)),
+            sem((S, links)), sem((S, links)), sem((S, half)), sem((S, half)),
+            sem((links,)), sem((links,)), sem((half,)), sem((half,)),
+            sem((links,)), sem((links,)), sem((half,)), sem((half,)),
+            sem((2 + SUB, line, 2)), sem((2 + SUB, line, 2)),
+            sem((S, SUB)), sem((S, SUB)), sem((S, SUB, half - 1)), sem((S, SUB, half - 1)),
         ],
         compiler_params=pltpu.CompilerParams(
             collective_id=0,
@@ -544,7 +603,7 @@
             vmem_limit_bytes=67_043_328,
         ),
     )(
-        tokens, norm_gain.reshape(1, D), queries, keys, values, out_weight,
+        tokens, norm_gain, queries, keys, values, out_weight,
         gate_weight, up_weight, down_weight,
     )
 

time: 307 us -> 277 us (0.902)
  Pallas kernels: 299 us -> 273 us
    pallas_call x1, Pallas kernels: 299 us -> 273 us  [shards(): pl.pallas_call(functools.partial(layer_kernel, S, T), out_shape=(jax.Shap...]
where the time goes in v1:
time: 277 us
  Pallas kernels  273 us (99%)
  local copies, waits for them, and re-layouts  3.37 us (1%)
    pallas_call x1, Pallas kernels, shards(): pl.pallas_call(functools.partial(layer_kernel, S, T), out_shape=(jax.Shap...  273 us

profile of v1, /device:TPU:0, one launch (start us, length us, event | category | flops | bytes accessed | tf_op | source)
XLA Modules:
  0.0 276.5 jit_solution(4541143555198857324)
XLA Ops:
  0.6 272.5 %shard_map.104 = (bf16[256,2048]{1,0:T(8,128)(2,1)}, bf16[256,2048]{1,0:T(8,128)(2,1)}) custom-call(bf16[256,2048]{1,0:T(8,128)(2,1)} %tok_ref.1, bf16[2048]{0:T(1024)(128)(2,1)} %gain_ref.1, bf16[256,2048]{1,0:T(8,128)(2,1)} %q_hbm.1, bf16[256,1024]{1,0:T(8,128)(2,1)} %k_hbm.1, bf16[256,1024]{1,0:T(8,128)(2,1)} %v_hbm.1, bf16[512,256]{1,0:T(8,128)(2,1)} %wo_hbm.1, ...), custom_call_target="tpu_custom_call" | custom-call | tf_op jit(solution)/shard_map/pallas_call | solution.py:569
  273.2 0.0 copy-start
  273.2 2.4 copy.13
  275.6 0.0 copy-done
  275.6 1.0 copy.14
Async XLA Ops:
  273.2 2.4 copy-start

commit v2 on v1

--- a/solution.py
+++ b/solution.py
@@ -28,7 +28,7 @@
     tok_ref, gain_ref, q_hbm, k_hbm, v_hbm, wo_hbm, gate_hbm, up_hbm, down_hbm,
     att_ref, out_ref,
     kv_all, q_all, qt_ref, acc_ref, attn_out, attn_full, wo_full, rows_all,
-    gate_full, up_full, down_full, pair_buf, rs_buf,
+    gate_full, up_full, down_full, pair_buf, rs_buf, gate_sum,
     loc, kvz_s, kvz_r, qz_s, qz_r, woz_s, woz_r, az_s, az_r,
     pk_s, pk_r, pkf_s, pkf_r, pw_s, pw_r, pwf_s, pwf_r, pr_s, pr_r, prf_s, prf_r,
     w_s, w_r, pair_s, pair_r, rs_s, rs_r,
@@ -414,10 +414,8 @@
         w_pass(m, 0)
     plane_corner(*row_plane)
     for d in range(1, S):
-        for m in (GATE, UP):
-            w_rest(m, d)
+        w_rest(GATE, d)
     w_loc[GATE].wait()
-    w_loc[UP].wait()
     plane_wait(*row_plane)
     plane_drain(*wo_plane)
     for g in range(S):
@@ -428,12 +426,26 @@
     def hidden_step(b, _):
         at = pl.ds(al(b * step_rows, step_rows), step_rows)
         x = rows_all[at, :]
-        gate = jnp.dot(x, gate_full[...], preferred_element_type=jnp.float32)
+        gate = gate_sum[at, :]
         up = jnp.dot(x, up_full[...], preferred_element_type=jnp.float32)
         wo_full[at, :F] = (gate / (1.0 + jnp.exp(-gate)) * up).astype(jnp.bfloat16)
         return 0
 
-    lax.fori_loop(0, half, hidden_step, 0)
+    def gate_step(b, _):
+        at = pl.ds(al(b * step_rows, step_rows), step_rows)
+        gate_sum[at, :] = jnp.dot(
+            rows_all[at, :], gate_full[...], preferred_element_type=jnp.float32
+        )
+        return 0
+
+    lax.fori_loop(0, half, gate_step, 0)
+    for d in range(1, S):
+        w_rest(UP, d)
+    w_loc[UP].wait()
+    lax.fori_loop(0, half // 2, hidden_step, 0)
+    for m in range(DOWN, DOWN + SUB):
+        w_pass(m, 1)
+    lax.fori_loop(half // 2, half, hidden_step, 0)
 
     near = jnp.minimum(s, S - 1 - s)
 
@@ -508,9 +520,9 @@
     steps = [(k, h) for k in range(S) for h in range(SUB)]
     for i, (k, h) in enumerate(steps):
         j = order(k)
-        if h == 0 and 1 <= max(k, 1) < S - 1 and k != 1:
+        if h == 0 and 2 <= k + 1 < S - 1:
             for m in range(DOWN, DOWN + SUB):
-                w_pass(m, max(k, 1))
+                w_pass(m, k + 1)
         if k >= 1:
             w_rest(DOWN + h, k)
         elif h == 0:
@@ -588,6 +600,7 @@
             pltpu.VMEM((F, D), bf16),
             pltpu.VMEM((S, SUB, half * rows, DG // SUB), bf16),
             pltpu.VMEM((S, SUB, half - 1, rows, DG // SUB), bf16),
+            pltpu.VMEM((T * rows, F), f32),
             sem((6 + SUB,)),
             sem((line, 2)), sem((line, 2)), sem((line,)), sem((line,)),
             sem((line,)), sem((line,)), sem((line,)), sem((line,)),

time: 277 us -> 277 us (level)
  no operation moved by 1% of the time
where the time goes in v2:
time: 277 us; the launch traced here: 276 us
  Pallas kernels  272 us (98%)
  local copies, waits for them, and re-layouts  3.37 us (1%)
    pallas_call x1, Pallas kernels, shards(): pl.pallas_call(functools.partial(layer_kernel, S, T), out_shape=(jax.Shap...  272 us

profile of v2, /device:TPU:0, one launch (start us, length us, event | category | flops | bytes accessed | tf_op | source)
XLA Modules:
  0.0 276.4 jit_solution(14018924067930394846)
XLA Ops:
  0.6 272.4 %shard_map.104 = (bf16[256,2048]{1,0:T(8,128)(2,1)}, bf16[256,2048]{1,0:T(8,128)(2,1)}) custom-call(bf16[256,2048]{1,0:T(8,128)(2,1)} %tok_ref.1, bf16[2048]{0:T(1024)(128)(2,1)} %gain_ref.1, bf16[256,2048]{1,0:T(8,128)(2,1)} %q_hbm.1, bf16[256,1024]{1,0:T(8,128)(2,1)} %k_hbm.1, bf16[256,1024]{1,0:T(8,128)(2,1)} %v_hbm.1, bf16[512,256]{1,0:T(8,128)(2,1)} %wo_hbm.1, ...), custom_call_target="tpu_custom_call" | custom-call | tf_op jit(solution)/shard_map/pallas_call | solution.py:581
  273.0 0.0 copy-start
  273.0 2.4 copy.13
  275.4 0.0 copy-done
  275.4 1.0 copy.14
Async XLA Ops:
  273.0 2.4 copy-start
